TPU v7x, 512 devices: a whole 4x4x16 slice. The times are simulated.
512 devices in a mesh: ctx: 32 (over x, z_lo), tp: 16 (over y, z_hi, core).
Axes of the slice: x: 4, y: 4, z: 16 (z_hi: 2, z_lo: 8; z = z_hi * 8 + z_lo), core: 2. Of those that a mesh axis runs over, the one named last changes fastest.
Arguments:
- queries: bfloat16 [8192, 8192], P('ctx', 'tp'), may hold values from -8 to 8
- keys: bfloat16 [8192, 1024], P('ctx'), may hold values from -7 to 7
- values: bfloat16 [8192, 1024], P('ctx'), may hold values from -6 to 6
- out_weight: bfloat16 [8192, 4096], P('tp'), may hold values from -0.25 to 0.25
- block_order: int32 [64], P('ctx'), may hold values from 0 to 63, each once
Outputs:
- projected: bfloat16 [8192, 4096], P('ctx', 'tp')
Inputs may be any that keep to these rules, and one draw needn't show every extreme that they name: `block_order`: every sequence block appears exactly once.
All inputs are finite; a program needn't handle non-finite values.
Results may differ from a plain program's by a relative error of at most 0.015.
Values may be sent and summed in bfloat16 or wider, within the bound.
A program may use at most 64 MiB of HBM per device.

v0:
```python
import math

import jax
import jax.numpy as jnp
from jax import lax
from jax.sharding import PartitionSpec as P

QUERY_HEADS = 64
KEY_VALUE_HEADS = 8
HEAD_SIZE = 128


def joined_along(blocks, dim):
    dims = list(blocks.shape[1:])
    dims[dim] *= blocks.shape[0]
    return jnp.moveaxis(blocks, 0, dim).reshape(dims)


def sent_to_all(array, axis):
    size = lax.axis_size(axis)
    return lax.all_to_all(
        jnp.broadcast_to(array[None], (size, *array.shape)), axis, 0, 0, tiled=True
    )


def gather_directly(array, axis, dim):
    return joined_along(sent_to_all(array, axis), dim)


def side_by_side(arrays, axis, dim, along):
    both = jnp.concatenate(arrays, axis=along)
    filled, at, done = (lax.all_gather(both, axis, axis=dim, tiled=True), 0, [])
    for a in arrays:
        done.append(lax.slice_in_dim(filled, at, at + a.shape[along], axis=along))
        at += a.shape[along]
    return tuple(done)


def shards(queries, keys, values, out_weight, block_order):
    tok_rows = queries.shape[0]
    block_len = tok_rows // 2
    heads_dev = queries.shape[1] // HEAD_SIZE
    group_size = QUERY_HEADS // KEY_VALUE_HEADS
    kv_heads = max(1, heads_dev // group_size)
    head_group = heads_dev // kv_heads
    whole_order = gather_directly(block_order, "ctx", 0)
    offsets = jnp.arange(block_len, dtype=jnp.int32)
    all_pos = (whole_order[:, None] * block_len + offsets[None, :]).reshape(-1)
    local_pos = (block_order[:, None] * block_len + offsets[None, :]).reshape(-1)
    first_head = lax.axis_index("tp") * heads_dev // group_size
    column_start = first_head * HEAD_SIZE
    own_keys = lax.dynamic_slice_in_dim(keys, column_start, kv_heads * HEAD_SIZE, 1)
    own_values = lax.dynamic_slice_in_dim(values, column_start, kv_heads * HEAD_SIZE, 1)
    scale = 1.0 / math.sqrt(HEAD_SIZE)
    query_heads = queries.reshape(tok_rows, kv_heads, head_group, HEAD_SIZE)

    def update(state, key_block, value_block, pos_block):
        run_max, run_sum, accum = state
        keyed = key_block.reshape(-1, kv_heads, HEAD_SIZE)
        valued = value_block.reshape(-1, kv_heads, HEAD_SIZE)
        scores = (
            jnp.einsum("tkgd,skd->kgts", query_heads, keyed, preferred_element_type=jnp.float32)
            * scale
        )
        visible = pos_block[None, None, None, :] <= local_pos[None, None, :, None]
        new_max = jnp.maximum(run_max, jnp.max(jnp.where(visible, scores, -1e30), axis=-1))
        weights = jnp.where(visible, jnp.exp(scores - new_max[..., None]), 0.0)
        factor = jnp.exp(run_max - new_max)
        run_sum = run_sum * factor + jnp.sum(weights, axis=-1)
        spread = jnp.transpose(factor, (2, 0, 1))[..., None]
        accum = accum * spread + jnp.einsum(
            "kgts,skd->tkgd",
            weights.astype(jnp.bfloat16),
            valued,
            preferred_element_type=jnp.float32,
        )
        return (new_max, run_sum, accum)

    start_state = (
        jnp.full((kv_heads, head_group, tok_rows), -1e30, jnp.float32),
        jnp.zeros((kv_heads, head_group, tok_rows), jnp.float32),
        jnp.zeros((tok_rows, kv_heads, head_group, HEAD_SIZE), jnp.float32),
    )
    piece_keys, piece_values = side_by_side((own_keys, own_values), "ctx", 0, 1)
    rows = piece_keys.shape[0]
    step_rows = math.gcd(rows, 512)

    def advance(carry, blocks):
        result = update(carry, blocks[0], blocks[1], blocks[2])
        return (result, None)

    stacked = (
        piece_keys.reshape(rows // step_rows, step_rows, -1),
        piece_values.reshape(rows // step_rows, step_rows, -1),
        all_pos.reshape(rows // step_rows, step_rows),
    )
    result, _ = lax.scan(advance, start_state, stacked)
    run_max, run_sum, accum = result
    totals = jnp.transpose(run_sum, (2, 0, 1))[..., None]
    attended = (accum / totals).reshape(tok_rows, heads_dev * HEAD_SIZE).astype(jnp.bfloat16)
    summed = lax.psum_scatter(
        lax.dot_general(
            out_weight, attended, (((0,), (1,)), ((), ())), preferred_element_type=jnp.float32
        ).astype(jnp.bfloat16),
        "tp",
        scatter_dimension=0,
        tiled=True,
    ).astype(jnp.float32)
    return summed.T.astype(jnp.bfloat16)


def solution(mesh):
    in_specs = (P("ctx", "tp"), P("ctx", None), P("ctx", None), P("tp", None), P("ctx"))
    out_specs = P("ctx", "tp")
    return jax.shard_map(shards, mesh=mesh, in_specs=in_specs, out_specs=out_specs, check_vma=False)
```

profile of v0, /device:TPU:1, one launch (start us, length us, event | category | flops | bytes accessed | tf_op | source)
XLA Modules:
  0.0 446.8 jit_solution(11177956828837318667)
XLA Ops:
  9.4 15.9 %all-to-all-start = ((s32[32,1,2]{2,1,0:T(1,128)}), s32[32,1,2]{2,1,0:T(1,128)S(1)}, u32[]{:S(2)}, u32[]{:S(2)}) async-start(s32[32,1,2]{2,1,0:T(1,128)} %broadcast_in_dim.43), calls=%async_computation | async-start | bytes 32768 | tf_op jit(solution)/shard_map/all_to_all | solution.py:21
  27.3 9.4 %all-to-all-done = s32[32,1,2]{2,1,0:T(1,128)S(1)} async-done(((s32[32,1,2]{2,1,0:T(1,128)}), s32[32,1,2]{2,1,0:T(1,128)S(1)}, u32[]{:S(2)}, u32[]{:S(2)}) %all-to-all-start) | async-done | bytes 288 | tf_op jit(solution)/shard_map/all_to_all | solution.py:21
  36.9 194.1 %all-gather.2.cloned.1.call-done = bf16[8192,256]{1,0:T(8,128)(2,1)} async-done(((bf16[256,256]{1,0:T(8,128)(2,1)}), bf16[8192,256]{1,0:T(8,128)(2,1)}) %all-gather.2.cloned.1.call-update) | async-done | bytes 4194320 | tf_op jit(solution)/shard_map/all_gather | solution.py:32
  231.0 4.5 fusion.26
  235.5 59.4 %while.15 = (s32[]{:T(128)}, f32[1,4,256]{2,1,0:T(4,128)S(1)}, f32[1,4,256]{2,1,0:T(4,128)S(1)}, f32[256,1,4,128]{0,3,2,1:T(8,128)S(1)}, s32[16,512]{1,0:T(8,128...) while((s32[]{:T(128)}, f32[1,4,256]{2,1,0:T(4,128)S(1)}, ...), condition=%wide.region_3.4_spmd.clone, body=%wide.region_0.3_spmd.clone.sunk | while | flops 274733312 | bytes 8463493 | solution.py:97
  235.7 1.4 fusion.37
  237.1 1.5 fusion.40
  239.4 1.4 fusion.37
  240.8 1.5 fusion.40
  243.1 1.4 fusion.37
  244.6 1.5 fusion.40
  246.9 1.4 fusion.37
  248.3 1.5 fusion.40
  250.6 1.4 fusion.37
  252.0 1.5 fusion.40
  254.3 1.4 fusion.37
  255.7 1.5 fusion.40
  258.0 1.4 fusion.37
  259.4 1.5 fusion.40
  261.7 1.4 fusion.37
  263.1 1.5 fusion.40
  265.4 1.4 fusion.37
  266.8 1.5 fusion.40
  270.6 1.5 fusion.40
  274.3 1.5 fusion.40
  278.0 1.5 fusion.40
  281.7 1.5 fusion.40
  285.4 1.5 fusion.40
  289.1 1.5 fusion.40
  292.8 1.5 fusion.40
  294.9 4.8 %fusion.25 = bf16[4096,256]{0,1:T(8,128)(2,1)} fusion(bf16[256,512]{0,1:T(8,128)(2,1)S(1)} %bitcast.103, bf16[512,4096]{1,0:T(8,128)(2,1)} %param.10), kind=kOutput, calls=%fused_computation.35 | convolution fusion | flops 1074790400 | bytes 6553600 | tf_op jit(solution)/shard_map/dot_general | solution.py:102
  299.8 140.2 %reduce-scatter.2.cloned.1.call-done = bf16[256,256]{0,1:T(8,128)(2,1)} async-done(((bf16[4096,256]{0,1:T(8,128)(2,1)}), bf16[256,256]{0,1:T(8,128)(2,1)}) %reduce-scatter.2.cloned.1.call-update) | async-done | bytes 131088 | tf_op jit(solution)/shard_map/reduce_scatter | solution.py:101
  (138 shorter events, 26.3 us)
Async XLA Ops:
  6.5 224.5 %all-gather.2.cloned.1.call-start = ((), (), s32[]{:S(2)}) async-start(), calls=%async_computation.2 | async-start | bytes 4325376 | tf_op jit(solution)/shard_map/all_gather | solution.py:32
  9.4 27.3 %all-to-all-start = ((s32[32,1,2]{2,1,0:T(1,128)}), s32[32,1,2]{2,1,0:T(1,128)S(1)}, u32[]{:S(2)}, u32[]{:S(2)}) async-start(s32[32,1,2]{2,1,0:T(1,128)} %broadcast_in_dim.43), calls=%async_computation | async-start | bytes 32768 | tf_op jit(solution)/shard_map/all_to_all | solution.py:21
  25.3 414.7 %reduce-scatter.2.cloned.1.call-start = ((), (), s32[]{:S(2)}) async-start(), calls=%async_computation.3 | async-start | bytes 2228224 | tf_op jit(solution)/shard_map/reduce_scatter | solution.py:101
Sparse Core Ops, SparseCore 0:
  9.4 221.5 all-gather.1
  299.9 140.0 reduce-scatter.1
where the time goes:
time: 448 us; the launch traced here: 447 us
  waiting for transfers between devices  344 us (77%)
  matrix products  51.7 us (12%)
  starting transfers between devices  16 us (4%)
  between operations  13.5 us (3%)
  other arithmetic  12.7 us (3%)
  local copies, waits for them, and re-layouts  8.21 us (2%)
    all_gather x1, waiting for transfers between devices, side_by_side(): filled, at, done = (lax.all_gather(both, axis, axis=dim, tiled=True), 0, [])  194 us
    reduce_scatter x1, waiting for transfers between devices, shards(): lax.psum_scatter(lax.dot_general(out_weight, attended, (((0,), (1,)), (()...  140 us
    dot_general x16, matrix products, update(): jnp.einsum('kgts,skd->tkgd', weights.astype(jnp.bfloat16), valued, prefer...  24.6 us
    dot_general x16, matrix products, update(): jnp.einsum('tkgd,skd->kgts', query_heads, keyed, preferred_element_type=j...  22.3 us
    all_to_all x1, starting transfers between devices, sent_to_all(): lax.all_to_all(jnp.broadcast_to(array[None], (size, *array.shape)), axis,...  15.9 us
    all_to_all x1, waiting for transfers between devices, sent_to_all(): lax.all_to_all(jnp.broadcast_to(array[None], (size, *array.shape)), axis,...  9.39 us
  transfers between devices with their start and end apart: 3, of which 3 were waited for; matrix products, arithmetic and copies ran while one was open for 1% of the time, Pallas kernels for 0%

commit v1 on v0

v1 whole, which is shorter than its diff:
```python
import functools
import math

import jax
import jax.numpy as jnp
from jax import lax
from jax.experimental import pallas as pl
from jax.experimental.pallas import tpu as pltpu
from jax.sharding import PartitionSpec as P

F32 = jnp.float32
BF = jnp.bfloat16
MESH = pl.DeviceIdType.MESH
HEAD = 128
BLK = 128
HEADS_DEV = 4
ROWS = 256
NX, NZL, NY = 4, 8, 4
LOG_SCALE = math.log2(math.e) / math.sqrt(HEAD)
LOW = -1e30
HIGH = 1e30

KROWS = BLK + 16
SLOT_ROWS = KROWS + HEAD
RIGHT = {1: 1, 2: 3, 3: 5, 4: 7}
LEFT = {1: 2, 2: 4, 3: 6}
GROUPS = [[0], [1, 2], [3, 4], [5, 6], [7]]


def beside(p):
    return [(dx, j, c) for j in GROUPS[p] for dx in (1, 2) for c in (0, 1)]


def column(p):
    return [(0, j, c) for j in GROUPS[p] for c in (0, 1)]


def across(p):
    return [(3, j, c) for j in GROUPS[p] for c in (0, 1)]


CHUNKS = [
    beside(0) + column(1),
    beside(1),
    column(2) + across(1),
    beside(2),
    column(3) + across(2),
    beside(3),
    across(3) + column(4) + across(0),
    beside(4) + across(4),
]
SLOT = {(0, 0, 0): 0, (0, 0, 1): 1}
for group in CHUNKS:
    for name in group:
        SLOT[name] = len(SLOT)
BASES = [SLOT[group[0]] for group in CHUNKS]


def kernel(
    q_hbm, k_hbm, v_hbm, w_hbm, order_ref, out_ref,
    kv, far, vtmp, vfar, q_ref, qt, s_ref, m_ref, acc, att, wbuf,
    keep, send1, recv1, send2, recv2, zsend, zpass, zrecv,
    load_sem, w_sem, send_sem, z_sem, x_sem, x2_sem, sib_sem, wx_sem, att_sem, r_sem, rs_sem,
):
    ctx = lax.axis_index("ctx")
    tp = lax.axis_index("tp")
    x, zl = ctx // NZL, ctx % NZL
    y, zh, core = tp // 4, (tp // 2) % 2, tp % 2
    zo = 1 - zh
    head = tp // 2
    far_head = y * 2 + zo

    def device(x_=None, zl_=None, y_=None, zh_=None, core_=None):
        x_ = x if x_ is None else x_
        zl_ = zl if zl_ is None else zl_
        y_ = y if y_ is None else y_
        zh_ = zh if zh_ is None else zh_
        core_ = core if core_ is None else core_
        return {"ctx": x_ * NZL + zl_, "tp": y_ * 4 + zh_ * 2 + core_}

    def along_z(step):
        z = (zh * NZL + zl + step + 2 * NZL) % (2 * NZL)
        return device(zl_=z % NZL, zh_=z // NZL)

    sibling = device(core_=1 - core)
    x_up, x_down = device(x_=(x + 1) % NX), device(x_=(x + NX - 1) % NX)
    y_near = y + 1 - 2 * (y % 2)
    y_wrap = NY - 1 - y
    y_diag = (y + 2) % NY
    y1, y2 = device(y_=y_near), device(y_=y_wrap)

    barrier = pltpu.get_barrier_semaphore()
    friends = [sibling, x_up, x_down, y1, y2] + [along_z(s) for s in (1, -1, 2, -2, 3, -3, 4, -4)]
    for friend in friends:
        pl.semaphore_signal(barrier, inc=1, device_id=friend, device_id_type=MESH)

    mine = pl.ds(pl.multiple_of(core * BLK, BLK), BLK)
    other = pl.ds(pl.multiple_of((1 - core) * BLK, BLK), BLK)
    own_cols = pl.ds(pl.multiple_of(head * HEAD, HEAD), HEAD)
    far_cols = pl.ds(pl.multiple_of(far_head * HEAD, HEAD), HEAD)
    loads = [
        pltpu.make_async_copy(v_hbm.at[mine, own_cols], vtmp.at[0], load_sem.at[0]),
        pltpu.make_async_copy(v_hbm.at[mine, far_cols], vfar, load_sem.at[1]),
        pltpu.make_async_copy(v_hbm.at[other, own_cols], vtmp.at[1], load_sem.at[2]),
        pltpu.make_async_copy(k_hbm.at[mine, own_cols], kv.at[0, 0:BLK], load_sem.at[3]),
        pltpu.make_async_copy(k_hbm.at[other, own_cols], kv.at[1, 0:BLK], load_sem.at[4]),
        pltpu.make_async_copy(k_hbm.at[mine, far_cols], far.at[0:BLK], load_sem.at[5]),
        pltpu.make_async_copy(q_hbm, q_ref, load_sem.at[6]),
    ]
    for load in loads:
        load.start()

    def w_cols(q, core_):
        return pl.ds(pl.multiple_of((q * 2 + core_) * ROWS, ROWS), ROWS)

    w_loads = [
        pltpu.make_async_copy(w_hbm.at[:, w_cols(q, core)], wbuf.at[q, 0:512], w_sem.at[q]) for q in range(8)
    ]
    place = [order_ref[0].astype(F32), order_ref[1].astype(F32)]
    my_place = order_ref[core].astype(F32)
    other_place = order_ref[1 - core].astype(F32)

    def transposed(v):
        return jnp.transpose(v.astype(F32)).astype(BF)

    kv[0, BLK:KROWS] = jnp.full((16, HEAD), my_place, F32).astype(BF)
    kv[1, BLK:KROWS] = jnp.full((16, HEAD), other_place, F32).astype(BF)
    far[BLK:KROWS] = jnp.full((16, HEAD), my_place, F32).astype(BF)
    loads[0].wait()
    kv[0, KROWS:SLOT_ROWS] = transposed(vtmp[0])
    loads[1].wait()
    far[KROWS:SLOT_ROWS] = transposed(vfar[...])
    loads[2].wait()
    kv[1, KROWS:SLOT_ROWS] = transposed(vtmp[1])
    for load in loads[3:]:
        load.wait()
    for load in w_loads:
        load.start()
    pl.semaphore_wait(barrier, len(friends))

    pending = []
    counter = [0]

    def send(src, dst, recv, target, when=None):
        copy = pltpu.make_async_remote_copy(
            src_ref=src, dst_ref=dst, send_sem=send_sem.at[counter[0]], recv_sem=recv,
            device_id=target, device_id_type=MESH,
        )
        counter[0] += 1
        pending.append((copy, when))
        if when is None:
            copy.start()
        else:
            pl.when(when)(copy.start)

    def arrived(dst, recv):
        pltpu.make_async_remote_copy(
            src_ref=dst, dst_ref=dst, send_sem=recv, recv_sem=recv, device_id=sibling, device_id_type=MESH
        ).wait_recv()

    def slot(dx, j, c):
        return kv.at[SLOT[(dx, j, c)]]

    def spread(j):
        send(slot(0, j, 0), slot(1, j, 0), x_sem.at[0, j], x_up)
        send(slot(0, j, 0), slot(2, j, 0), x_sem.at[1, j], x_down)

    def share(dx, j):
        send(slot(dx, j, 0), slot(dx, j, 1), sib_sem.at[dx, j], sibling)

    def column_event(p):
        for j in GROUPS[p]:
            arrived(slot(0, j, 0), z_sem.at[j])
            for d in (1, 2, 3):
                if RIGHT[d] == j:
                    n = RIGHT[d + 1]
                    send(slot(0, j, 0), slot(0, n, 0), z_sem.at[n], along_z(1), zl < NZL - 1)
            for d in (1, 2):
                if LEFT[d] == j:
                    n = LEFT[d + 1]
                    send(slot(0, j, 0), slot(0, n, 0), z_sem.at[n], along_z(-1), zl > 0)
            spread(j)
            share(0, j)

    def beside_event(p):
        for j in GROUPS[p]:
            arrived(slot(1, j, 0), x_sem.at[0, j])
            send(slot(1, j, 0).at[0:KROWS], slot(3, j, 0).at[0:KROWS], x2_sem.at[0, j], x_up)
            arrived(slot(2, j, 0), x_sem.at[1, j])
            send(
                slot(2, j, 0).at[KROWS:SLOT_ROWS], slot(3, j, 0).at[KROWS:SLOT_ROWS], x2_sem.at[1, j], x_down
            )
            share(1, j)
            share(2, j)

    def across_event(p):
        for j in GROUPS[p]:
            arrived(slot(3, j, 0).at[0:KROWS], x2_sem.at[0, j])
            arrived(slot(3, j, 0).at[KROWS:SLOT_ROWS], x2_sem.at[1, j])
            share(3, j)

    def w_send(q):
        send(w_hbm.at[:, w_cols(q, 1 - core)], wbuf.at[q, 512:1024], wx_sem.at[q], sibling)

    def prepare_queries():
        for h in range(HEADS_DEV):
            t = jnp.transpose(q_ref[:, h * HEAD : (h + 1) * HEAD].astype(F32)) * LOG_SCALE
            top = t.astype(BF)
            qt[h, 0:HEAD] = top
            qt[h, HEAD : 2 * HEAD] = (t - top.astype(F32)).astype(BF)

    q_place = jnp.concatenate([jnp.full((1, BLK), place[0], F32), jnp.full((1, BLK), place[1], F32)], axis=1)

    def keys_values(base, count):
        ks, vs = [], []
        for i in range(count):
            k = kv[base + i, 0:BLK]
            ks.append(jnp.concatenate([k, k], axis=1))
            vs.append(kv[base + i, KROWS:SLOT_ROWS])
        values = jnp.concatenate([jnp.concatenate(vs, axis=1), jnp.ones((16, count * BLK), BF)], axis=0)
        return jnp.concatenate(ks, axis=0), values

    def own_chunk():
        keys, values = keys_values(0, 2)
        rows = lax.broadcasted_iota(jnp.int32, (BLK, ROWS), 0).astype(F32)
        lanes = (lax.broadcasted_iota(jnp.int32, (1, ROWS), 1) % BLK).astype(F32)
        q_pos = q_place * BLK + lanes
        seen = [rows + my_place * BLK <= q_pos, rows + other_place * BLK <= q_pos]
        for h in range(HEADS_DEV):
            s = jnp.dot(keys, qt[h], preferred_element_type=F32)
            parts = [jnp.where(seen[i], s[i * BLK : (i + 1) * BLK], LOW) for i in range(2)]
            top = jnp.maximum(
                jnp.max(parts[0], axis=0, keepdims=True), jnp.max(parts[1], axis=0, keepdims=True)
            )
            weights = jnp.concatenate([jnp.exp2(part - top).astype(BF) for part in parts], axis=0)
            acc[h] = jnp.dot(values, weights, preferred_element_type=F32)
            m_ref[h, 0:1] = top

    def chunk(n):
        base, count = BASES[n], len(CHUNKS[n])
        for dx, j, c in CHUNKS[n]:
            if c == 1:
                arrived(slot(dx, j, 1), sib_sem.at[dx, j])
        keys, values = keys_values(base, count)
        seen = []
        for i in range(count):
            p = kv[base + i, BLK:KROWS].astype(F32)[0:1]
            seen.append(jnp.concatenate([p, p], axis=1) < q_place)
        for h in range(HEADS_DEV):
            s_ref[h, 0 : count * BLK] = jnp.dot(keys, qt[h], preferred_element_type=F32)
        for h in range(HEADS_DEV):
            old = m_ref[h, 0:1]
            top = old
            for i in range(count):
                high = jnp.max(s_ref[h, i * BLK : (i + 1) * BLK], axis=0, keepdims=True)
                top = jnp.maximum(top, jnp.where(seen[i], high, LOW))
            weights = jnp.concatenate(
                [
                    jnp.exp2(s_ref[h, i * BLK : (i + 1) * BLK] - jnp.where(seen[i], top, HIGH)).astype(BF)
                    for i in range(count)
                ],
                axis=0,
            )
            acc[h] = acc[h] * jnp.exp2(old - top) + jnp.dot(values, weights, preferred_element_type=F32)
            m_ref[h, 0:1] = top

    spread(0)
    send(slot(0, 0, 0), slot(0, RIGHT[1], 0), z_sem.at[RIGHT[1]], along_z(1), zl < NZL - 1)
    send(slot(0, 0, 0), slot(0, LEFT[1], 0), z_sem.at[LEFT[1]], along_z(-1), zl > 0)
    for d in (1, 2, 3, 4):
        send(far, slot(0, RIGHT[d], 0), z_sem.at[RIGHT[d]], along_z(d), zl == NZL - d)
    for d in (1, 2, 3):
        send(far, slot(0, LEFT[d], 0), z_sem.at[LEFT[d]], along_z(-d), zl == d - 1)

    prepare_queries()
    own_chunk()
    beside_event(0)
    column_event(1)
    w_send(0)
    w_send(1)
    across_event(0)
    chunk(0)
    column_event(2)
    beside_event(1)
    chunk(1)
    across_event(1)
    w_send(2)
    w_send(3)
    chunk(2)
    column_event(3)
    beside_event(2)
    chunk(3)
    across_event(2)
    w_send(4)
    w_send(5)
    chunk(4)
    column_event(4)
    beside_event(3)
    chunk(5)
    across_event(3)
    w_send(6)
    w_send(7)
    beside_event(4)
    chunk(6)
    across_event(4)
    chunk(7)

    for h in range(HEADS_DEV):
        a = acc[h]
        att[:, h * HEAD : (h + 1) * HEAD] = jnp.transpose(a[0:HEAD] / a[HEAD : HEAD + 1]).astype(BF)
    send(att.at[:, 0:512], att.at[:, 512:1024], att_sem, sibling)
    for load in w_loads:
        load.wait()
    for q in range(8):
        arrived(wbuf.at[q, 512:1024], wx_sem.at[q])
    arrived(att.at[:, 512:1024], att_sem)

    def product(y_, zz):
        q = y_ * 2 + zz
        return jnp.dot(att[...], wbuf[q], preferred_element_type=F32)

    half = ROWS // 2
    first_to = [y1, y2]
    second_to = [y2, y1]

    def first_products(n, zz):
        d = product(y_diag, zz)
        send1[n, 0, 1] = d[0:half].astype(BF)
        send1[n, 1, 1] = d[half:ROWS].astype(BF)
        a = product(y_near, zz)
        send1[n, 0, 0] = a[0:half].astype(BF)
        keep[n, 1, 1] = a[half:ROWS]
        b = product(y_wrap, zz)
        send1[n, 1, 0] = b[half:ROWS].astype(BF)
        keep[n, 0, 1] = b[0:half]
        c = product(y, zz)
        keep[n, 0, 0] = c[0:half]
        keep[n, 1, 0] = c[half:ROWS]

    def first_sends(n):
        for f in range(2):
            send(send1.at[n, f], recv1.at[n, f], r_sem.at[0, n, f], first_to[f])

    def second_sends(n):
        for f in range(2):
            arrived(recv1.at[n, f], r_sem.at[0, n, f])
            send2[n, f] = (keep[n, f, 1] + recv1[n, f, 1].astype(F32)).astype(BF)
            send(send2.at[n, f], recv2.at[n, f], r_sem.at[1, n, f], second_to[f])

    def column_sum(n, f):
        arrived(recv2.at[n, f], r_sem.at[1, n, f])
        return keep[n, f, 0] + recv1[n, f, 0].astype(F32) + recv2[n, f].astype(F32)

    z_four = [along_z(4), along_z(-4)]
    first_products(0, zo)
    first_sends(0)
    first_products(1, zh)
    second_sends(0)
    first_sends(1)
    for f in range(2):
        zsend[f] = column_sum(0, f).astype(BF)
        send(zsend.at[f], zpass.at[f], rs_sem.at[0, f], z_four[f])
    second_sends(1)
    for f in range(2):
        arrived(zpass.at[f], rs_sem.at[0, f])
        send(zpass.at[f], zrecv.at[f], rs_sem.at[1, f], z_four[f])
    for f in range(2):
        keep[1, f, 0] = column_sum(1, f)
    for f in range(2):
        arrived(zrecv.at[f], rs_sem.at[1, f])
        out_ref[f * half : (f + 1) * half] = (keep[1, f, 0] + zrecv[f].astype(F32)).astype(BF)

    for copy, when in pending:
        if when is None:
            copy.wait_send()
        else:
            pl.when(when)(copy.wait_send)


SENDS = 192


def shards(queries, keys, values, out_weight, block_order):
    any_spec = pl.BlockSpec(memory_space=pl.ANY)
    half = ROWS // 2
    dma = pltpu.SemaphoreType.DMA
    return pl.pallas_call(
        kernel,
        out_shape=jax.ShapeDtypeStruct((ROWS, ROWS), BF),
        in_specs=[any_spec] * 4 + [pl.BlockSpec(memory_space=pltpu.SMEM)],
        out_specs=pl.BlockSpec(memory_space=pltpu.VMEM),
        scratch_shapes=[
            pltpu.VMEM((64, SLOT_ROWS, HEAD), BF),
            pltpu.VMEM((SLOT_ROWS, HEAD), BF),
            pltpu.VMEM((2, BLK, HEAD), BF),
            pltpu.VMEM((BLK, HEAD), BF),
            pltpu.VMEM((ROWS, HEADS_DEV * HEAD), BF),
            pltpu.VMEM((HEADS_DEV, 2 * HEAD, ROWS), BF),
            pltpu.VMEM((HEADS_DEV, 8 * BLK, ROWS), F32),
            pltpu.VMEM((HEADS_DEV, 8, ROWS), F32),
            pltpu.VMEM((HEADS_DEV, HEAD + 16, ROWS), F32),
            pltpu.VMEM((ROWS, 1024), BF),
            pltpu.VMEM((8, 1024, ROWS), BF),
            pltpu.VMEM((2, 2, 2, half, ROWS), F32),
            pltpu.VMEM((2, 2, 2, half, ROWS), BF),
            pltpu.VMEM((2, 2, 2, half, ROWS), BF),
            pltpu.VMEM((2, 2, half, ROWS), BF),
            pltpu.VMEM((2, 2, half, ROWS), BF),
            pltpu.VMEM((2, half, ROWS), BF),
            pltpu.VMEM((2, half, ROWS), BF),
            pltpu.VMEM((2, half, ROWS), BF),
            dma((7,)),
            dma((8,)),
            dma((SENDS,)),
            dma((8,)),
            dma((2, 8)),
            dma((2, 8)),
            dma((4, 8)),
            dma((8,)),
            dma,
            dma((2, 2, 2)),
            dma((2, 2)),
        ],
        compiler_params=pltpu.CompilerParams(
            collective_id=0, has_side_effects=True, vmem_limit_bytes=56 * 2**20
        ),
    )(queries, keys, values, out_weight, block_order)


def solution(mesh):
    in_specs = (P("ctx", "tp"), P("ctx", None), P("ctx", None), P("tp", None), P("ctx"))
    out_specs = P("ctx", "tp")
    return jax.shard_map(shards, mesh=mesh, in_specs=in_specs, out_specs=out_specs, check_vma=False)
```

time: 448 us -> 87 us (0.19)
  the two profiles are of different devices: /device:TPU:1 before, /device:TPU:8 now
where the time goes in v1:
time: 87 us; the launch traced here: 86.8 us
  Pallas kernels  85.3 us (98%)
  local copies, waits for them, and re-layouts  1.57 us (2%)
    pallas_call x1, Pallas kernels, shards(): pl.pallas_call(kernel, out_shape=jax.ShapeDtypeStruct((ROWS, ROWS), BF),...  85.3 us

profile of v1, /device:TPU:8, one launch (start us, length us, event | category | flops | bytes accessed | tf_op | source)
XLA Modules:
  0.0 86.8 jit_solution(17756068532501599578)
XLA Ops:
  0.0 85.3 %shard_map.55 = bf16[256,256]{1,0:T(8,128)(2,1)} custom-call(bf16[256,512]{1,0:T(8,128)(2,1)} %q_hbm.1, bf16[256,1024]{1,0:T(8,128)(2,1)} %k_hbm.1, bf16[256,1024]{1,0:T(8,128)(2,1)} %v_hbm.1, bf16[512,4096]{1,0:T(8,128)(2,1)} %w_hbm.1, s32[2]{0:T(128)} %order_ref.1), custom_call_target="tpu_custom_call" | custom-call | tf_op jit(solution)/shard_map/pallas_call | solution.py:387
  85.3 1.6 %copy.7 = bf16[256,256]{1,0:T(8,128)(2,1)} copy(bf16[256,256]{1,0:T(8,128)(2,1)} %shard_map.55) | data formatting | bytes 262144

commit v2 on v1

v2 whole, which is shorter than its diff:
```python
import functools
import math

import jax
import jax.numpy as jnp
from jax import lax
from jax.experimental import pallas as pl
from jax.experimental.pallas import tpu as pltpu
from jax.sharding import PartitionSpec as P

F32 = jnp.float32
BF = jnp.bfloat16
MESH = pl.DeviceIdType.MESH
HEAD = 128
BLK = 128
HEADS_DEV = 4
ROWS = 256
NX, NZL, NY = 4, 8, 4
LOG_SCALE = math.log2(math.e) / math.sqrt(HEAD)
LOW = -1e30
HIGH = 1e30

KROWS = BLK + 16
SLOT_ROWS = KROWS + HEAD
GROUPS = [[0], [1, 2], [3, 4], [5, 6], [7]]


def group(kind, p):
    side = (1, 2) if kind == "beside" else (0,) if kind == "column" else (3,)
    return [(dx, j, c) for c in (0, 1) for j in GROUPS[p] for dx in side]


CHUNKS = [
    [("beside", 0), ("column", 1)],
    [("beside", 1)],
    [("column", 2), ("across", 1)],
    [("beside", 2)],
    [("column", 3), ("across", 2)],
    [("beside", 3)],
    [("across", 3), ("column", 4), ("across", 0)],
    [("beside", 4), ("across", 4)],
]
SLOT = {(0, 0, 0): 1, (0, 0, 1): 2}
SPANS = []
for parts in CHUNKS:
    first = len(SLOT) + 1
    for part in parts:
        for name in group(*part):
            SLOT[name] = len(SLOT) + 1
    SPANS.append((first, len(SLOT) + 1 - first))
SLOTS = len(SLOT) + 1


def kernel(
    q_hbm, k_hbm, v_hbm, w_hbm, order_ref, out_ref,
    kv, vtmp, q_ref, qt, s_ref, m_ref, acc, att, wbuf,
    keep, send1, recv1, send2, recv2, zsend, zrecv,
    load_sem, w_sem, send_sem, z_sem, x_sem, x2_sem, sib_sem, wx_sem, att_sem, att_sent, r_sem, r_sent, z8_sem, z8_sent,
):
    ctx = lax.axis_index("ctx")
    tp = lax.axis_index("tp")
    x, zl = ctx // NZL, ctx % NZL
    y, zh, core = tp // 4, (tp // 2) % 2, tp % 2
    zo = 1 - zh
    head = tp // 2
    far_head = y * 2 + zo

    def device(x_=None, zl_=None, y_=None, zh_=None, core_=None):
        x_ = x if x_ is None else x_
        zl_ = zl if zl_ is None else zl_
        y_ = y if y_ is None else y_
        zh_ = zh if zh_ is None else zh_
        core_ = core if core_ is None else core_
        return {"ctx": x_ * NZL + zl_, "tp": y_ * 4 + zh_ * 2 + core_}

    def along_z(step):
        z = (zh * NZL + zl + step + 2 * NZL) % (2 * NZL)
        return device(zl_=z % NZL, zh_=z // NZL)

    sibling = device(core_=1 - core)
    x_over, z_over = device(x_=(x + 2) % NX), device(zh_=zo)
    x_up, x_down = device(x_=(x + 1) % NX), device(x_=(x + NX - 1) % NX)
    y_near = y + 1 - 2 * (y % 2)
    y_wrap = NY - 1 - y
    y_diag = (y + 2) % NY
    y1, y2 = device(y_=y_near), device(y_=y_wrap)

    barrier = pltpu.get_barrier_semaphore()
    friends = [sibling, x_up, x_down, x_over, y1, y2, z_over]
    friends += [along_z(s) for s in (1, -1, 2, -2, 3, -3, 4, -4)]
    for friend in friends:
        pl.semaphore_signal(barrier, inc=1, device_id=friend, device_id_type=MESH)

    mine = pl.ds(pl.multiple_of(core * BLK, BLK), BLK)
    other = pl.ds(pl.multiple_of((1 - core) * BLK, BLK), BLK)
    own_cols = pl.ds(pl.multiple_of(head * HEAD, HEAD), HEAD)
    far_cols = pl.ds(pl.multiple_of(far_head * HEAD, HEAD), HEAD)
    loads = [
        pltpu.make_async_copy(v_hbm.at[mine, own_cols], vtmp.at[0], load_sem.at[0]),
        pltpu.make_async_copy(v_hbm.at[mine, far_cols], vtmp.at[1], load_sem.at[1]),
        pltpu.make_async_copy(v_hbm.at[other, own_cols], vtmp.at[2], load_sem.at[2]),
        pltpu.make_async_copy(k_hbm.at[mine, own_cols], kv.at[1, 0:BLK], load_sem.at[3]),
        pltpu.make_async_copy(k_hbm.at[mine, far_cols], kv.at[0, 0:BLK], load_sem.at[4]),
        pltpu.make_async_copy(k_hbm.at[other, own_cols], kv.at[2, 0:BLK], load_sem.at[5]),
        pltpu.make_async_copy(q_hbm, q_ref, load_sem.at[6]),
    ]
    for load in loads:
        load.start()

    def w_cols(q, core_):
        return pl.ds(pl.multiple_of((q * 2 + core_) * ROWS, ROWS), ROWS)

    def w_loaded():
        whole = wbuf.at[:, 0:512]
        return pltpu.make_async_copy(whole, whole, w_sem)

    place = [order_ref[0].astype(F32), order_ref[1].astype(F32)]
    my_place = order_ref[core].astype(F32)
    other_place = order_ref[1 - core].astype(F32)

    def transposed(v):
        return jnp.transpose(v.astype(F32)).astype(BF)

    for i, (which, load) in enumerate([(my_place, 1), (my_place, 0), (other_place, 2)]):
        kv[load, BLK:KROWS] = jnp.full((16, HEAD), which, F32).astype(BF)
        loads[i].wait()
        kv[load, KROWS:SLOT_ROWS] = transposed(vtmp[i])
    for load in loads[3:]:
        load.wait()
    for q in range(8):
        pltpu.make_async_copy(w_hbm.at[:, w_cols(q, core)], wbuf.at[q, 0:512], w_sem).start()
    pl.semaphore_wait(barrier, len(friends))

    def send(src, dst, recv, target, sent=None):
        pltpu.make_async_remote_copy(
            src_ref=src, dst_ref=dst, send_sem=send_sem if sent is None else sent, recv_sem=recv,
            device_id=target, device_id_type=MESH,
        ).start()

    def landed(ref, sem):
        return pltpu.make_async_remote_copy(
            src_ref=ref, dst_ref=ref, send_sem=sem, recv_sem=sem, device_id=sibling, device_id_type=MESH
        )

    def arrived(ref, sem):
        landed(ref, sem).wait_recv()

    def slot(dx, j, c):
        return kv.at[SLOT[(dx, j, c)]]

    def part(kind, p, c):
        names = group(kind, p)
        count = len(names) // 2
        return kv.at[pl.ds(SLOT[names[c * count]], count)]

    KINDS = {"column": 0, "beside": 1, "across": 2}

    def spread(p, j):
        send(slot(0, j, 0), slot(1, j, 0), x_sem.at[p], x_up)
        send(slot(0, j, 0), slot(2, j, 0), x_sem.at[p], x_down)
        send(slot(0, j, 0), slot(3, j, 0), x2_sem.at[p], x_over)

    def share(kind, p):
        send(part(kind, p, 0), part(kind, p, 1), sib_sem.at[KINDS[kind], p], sibling)

    def column_event(p):
        for j in GROUPS[p]:
            arrived(slot(0, j, 0), z_sem.at[j])
            spread(p, j)
        share("column", p)

    def beside_event(p):
        arrived(part("beside", p, 0), x_sem.at[p])
        share("beside", p)

    def across_event(p):
        arrived(part("across", p, 0), x2_sem.at[p])
        share("across", p)

    def w_send(q):
        send(w_hbm.at[:, w_cols(q, 1 - core)], wbuf.at[q, 512:1024], wx_sem.at[0], sibling, wx_sem.at[1])

    def prepare_queries():
        for h in range(HEADS_DEV):
            t = jnp.transpose(q_ref[:, h * HEAD : (h + 1) * HEAD].astype(F32)) * LOG_SCALE
            top = t.astype(BF)
            qt[h, 0:HEAD] = top
            qt[h, HEAD : 2 * HEAD] = (t - top.astype(F32)).astype(BF)

    q_place = jnp.concatenate([jnp.full((1, BLK), place[0], F32), jnp.full((1, BLK), place[1], F32)], axis=1)

    def keys_values(base, count):
        ks, vs = [], []
        for i in range(count):
            k = kv[base + i, 0:BLK]
            ks.append(jnp.concatenate([k, k], axis=1))
            vs.append(kv[base + i, KROWS:SLOT_ROWS])
        values = jnp.concatenate([jnp.concatenate(vs, axis=1), jnp.ones((16, count * BLK), BF)], axis=0)
        return jnp.concatenate(ks, axis=0), values

    def own_chunk():
        keys, values = keys_values(1, 2)
        rows = lax.broadcasted_iota(jnp.int32, (BLK, ROWS), 0).astype(F32)
        lanes = (lax.broadcasted_iota(jnp.int32, (1, ROWS), 1) % BLK).astype(F32)
        q_pos = q_place * BLK + lanes
        seen = [rows + my_place * BLK <= q_pos, rows + other_place * BLK <= q_pos]
        for h in range(HEADS_DEV):
            s = jnp.dot(keys, qt[h], preferred_element_type=F32)
            parts = [jnp.where(seen[i], s[i * BLK : (i + 1) * BLK], LOW) for i in range(2)]
            top = jnp.maximum(
                jnp.max(parts[0], axis=0, keepdims=True), jnp.max(parts[1], axis=0, keepdims=True)
            )
            weights = jnp.concatenate([jnp.exp2(part - top).astype(BF) for part in parts], axis=0)
            acc[h] = jnp.dot(values, weights, preferred_element_type=F32)
            m_ref[h, 0:1] = top

    def chunk(n):
        base, count = SPANS[n]
        for kind, p in CHUNKS[n]:
            arrived(part(kind, p, 1), sib_sem.at[KINDS[kind], p])
        keys, values = keys_values(base, count)
        seen = []
        for i in range(count):
            p = kv[base + i, BLK:KROWS].astype(F32)[0:1]
            seen.append(jnp.concatenate([p, p], axis=1) < q_place)
        for h in range(HEADS_DEV):
            s_ref[h, 0 : count * BLK] = jnp.dot(keys, qt[h], preferred_element_type=F32)
        for h in range(HEADS_DEV):
            old = m_ref[h, 0:1]
            top = old
            for i in range(count):
                high = jnp.max(s_ref[h, i * BLK : (i + 1) * BLK], axis=0, keepdims=True)
                top = jnp.maximum(top, jnp.where(seen[i], high, LOW))
            weights = jnp.concatenate(
                [
                    jnp.exp2(s_ref[h, i * BLK : (i + 1) * BLK] - jnp.where(seen[i], top, HIGH)).astype(BF)
                    for i in range(count)
                ],
                axis=0,
            )
            acc[h] = acc[h] * jnp.exp2(old - top) + jnp.dot(values, weights, preferred_element_type=F32)
            m_ref[h, 0:1] = top

    def for_step(step):
        return kv.at[jnp.where((zl + step >= 0) & (zl + step < NZL), 1, 0)]

    def right(d):
        j = 2 * d - 1
        send(for_step(d), slot(0, j, 0), z_sem.at[j], along_z(d))

    def left(d):
        j = 2 * d
        send(for_step(-d), slot(0, j, 0), z_sem.at[j], along_z(-d))

    right(1)
    left(1)
    spread(0, 0)
    right(2)
    left(2)
    right(3)
    left(3)
    send(for_step(4).at[0:KROWS], slot(0, 7, 0).at[0:KROWS], z_sem.at[7], along_z(4))
    send(for_step(-4).at[KROWS:SLOT_ROWS], slot(0, 7, 0).at[KROWS:SLOT_ROWS], z_sem.at[7], along_z(-4))

    prepare_queries()
    own_chunk()
    column_event(1)
    beside_event(0)
    across_event(0)
    w_send(0)
    w_send(1)
    chunk(0)
    column_event(2)
    beside_event(1)
    w_send(2)
    w_send(3)
    chunk(1)
    column_event(3)
    across_event(1)
    w_send(4)
    w_send(5)
    chunk(2)
    column_event(4)
    beside_event(2)
    w_send(6)
    w_send(7)
    chunk(3)
    across_event(2)
    chunk(4)
    beside_event(3)
    chunk(5)
    across_event(3)
    chunk(6)
    beside_event(4)
    across_event(4)
    chunk(7)

    for h in range(HEADS_DEV):
        a = acc[h]
        att[:, h * HEAD : (h + 1) * HEAD] = jnp.transpose(a[0:HEAD] / a[HEAD : HEAD + 1]).astype(BF)
    send(att.at[:, 0:512], att.at[:, 512:1024], att_sem, sibling, att_sent)
    w_loaded().wait()
    arrived(wbuf.at[:, 512:1024], wx_sem.at[0])
    arrived(att.at[:, 512:1024], att_sem)

    def product(y_, zz):
        q = y_ * 2 + zz
        return jnp.dot(att[...], wbuf[q], preferred_element_type=F32)

    half = ROWS // 2
    first_to = [y1, y2]
    second_to = [y2, y1]

    def first_products(n, zz):
        d = product(y_diag, zz)
        send1[n, 0, 1] = d[0:half].astype(BF)
        send1[n, 1, 1] = d[half:ROWS].astype(BF)
        a = product(y_near, zz)
        send1[n, 0, 0] = a[0:half].astype(BF)
        keep[n, 1, 1] = a[half:ROWS]
        b = product(y_wrap, zz)
        send1[n, 1, 0] = b[half:ROWS].astype(BF)
        keep[n, 0, 1] = b[0:half]
        c = product(y, zz)
        keep[n, 0, 0] = c[0:half]
        keep[n, 1, 0] = c[half:ROWS]

    piece = half // 2

    def rows(u):
        return pl.ds(u * piece, piece)

    def first_send(n, f, u):
        send(
            send1.at[n, f, :, rows(u)], recv1.at[n, f, :, rows(u)], r_sem.at[0, n, f, u], first_to[f], r_sent.at[0]
        )

    def second_send(n, f, u):
        arrived(recv1.at[n, f, :, rows(u)], r_sem.at[0, n, f, u])
        send2[n, f, rows(u)] = (keep[n, f, 1, rows(u)] + recv1[n, f, 1, rows(u)].astype(F32)).astype(BF)
        send(send2.at[n, f, rows(u)], recv2.at[n, f, rows(u)], r_sem.at[1, n, f, u], second_to[f], r_sent.at[1])

    def column_sum(n, f, u):
        arrived(recv2.at[n, f, rows(u)], r_sem.at[1, n, f, u])
        return keep[n, f, 0, rows(u)] + recv1[n, f, 0, rows(u)].astype(F32) + recv2[n, f, rows(u)].astype(F32)

    steps = [(f, u) for u in range(2) for f in range(2)]
    first_products(0, zo)
    for f, u in steps:
        first_send(0, f, u)
    first_products(1, zh)
    for f, u in steps:
        second_send(0, f, u)
    for f, u in steps:
        first_send(1, f, u)
    for f, u in steps:
        zsend[f, rows(u)] = column_sum(0, f, u).astype(BF)
        send(zsend.at[f, rows(u)], zrecv.at[f, rows(u)], z8_sem.at[f, u], z_over, z8_sent)
    for f, u in steps:
        second_send(1, f, u)
    for f, u in steps:
        keep[1, f, 0, rows(u)] = column_sum(1, f, u)
    for f, u in steps:
        arrived(zrecv.at[f, rows(u)], z8_sem.at[f, u])
        out_ref[pl.ds(f * half + u * piece, piece)] = (
            keep[1, f, 0, rows(u)] + zrecv[f, rows(u)].astype(F32)
        ).astype(BF)

    landed(kv.at[pl.ds(0, 62)], send_sem).wait_send()
    landed(wbuf.at[:, 512:1024], wx_sem.at[1]).wait_send()
    landed(att.at[:, 0:512], att_sent).wait_send()
    landed(send1, r_sent.at[0]).wait_send()
    landed(send2, r_sent.at[1]).wait_send()
    landed(zsend, z8_sent).wait_send()


def shards(queries, keys, values, out_weight, block_order):
    any_spec = pl.BlockSpec(memory_space=pl.ANY)
    half = ROWS // 2
    dma = pltpu.SemaphoreType.DMA
    return pl.pallas_call(
        kernel,
        out_shape=jax.ShapeDtypeStruct((ROWS, ROWS), BF),
        in_specs=[any_spec] * 4 + [pl.BlockSpec(memory_space=pltpu.SMEM)],
        out_specs=pl.BlockSpec(memory_space=pltpu.VMEM),
        scratch_shapes=[
            pltpu.VMEM((SLOTS, SLOT_ROWS, HEAD), BF),
            pltpu.VMEM((3, BLK, HEAD), BF),
            pltpu.VMEM((ROWS, HEADS_DEV * HEAD), BF),
            pltpu.VMEM((HEADS_DEV, 2 * HEAD, ROWS), BF),
            pltpu.VMEM((HEADS_DEV, 8 * BLK, ROWS), F32),
            pltpu.VMEM((HEADS_DEV, 8, ROWS), F32),
            pltpu.VMEM((HEADS_DEV, HEAD + 16, ROWS), F32),
            pltpu.VMEM((ROWS, 1024), BF),
            pltpu.VMEM((8, 1024, ROWS), BF),
            pltpu.VMEM((2, 2, 2, half, ROWS), F32),
            pltpu.VMEM((2, 2, 2, half, ROWS), BF),
            pltpu.VMEM((2, 2, 2, half, ROWS), BF),
            pltpu.VMEM((2, 2, half, ROWS), BF),
            pltpu.VMEM((2, 2, half, ROWS), BF),
            pltpu.VMEM((2, half, ROWS), BF),
            pltpu.VMEM((2, half, ROWS), BF),
            dma((7,)),
            dma,
            dma,
            dma((8,)),
            dma((5,)),
            dma((5,)),
            dma((3, 5)),
            dma((2,)),
            dma,
            dma,
            dma((2, 2, 2, 2)),
            dma((2,)),
            dma((2, 2)),
            dma,
        ],
        compiler_params=pltpu.CompilerParams(
            collective_id=0, has_side_effects=True, vmem_limit_bytes=56 * 2**20
        ),
    )(queries, keys, values, out_weight, block_order)


def solution(mesh):
    in_specs = (P("ctx", "tp"), P("ctx", None), P("ctx", None), P("tp", None), P("ctx"))
    out_specs = P("ctx", "tp")
    return jax.shard_map(shards, mesh=mesh, in_specs=in_specs, out_specs=out_specs, check_vma=False)
```

time: 87 us -> 74.6 us (0.86)
  the two profiles are of different devices: /device:TPU:8 before, /device:TPU:2 now
where the time goes in v2:
time: 74.6 us; the launch traced here: 74.5 us
  Pallas kernels  72.9 us (98%)
  local copies, waits for them, and re-layouts  1.57 us (2%)
    pallas_call x1, Pallas kernels, shards(): pl.pallas_call(kernel, out_shape=jax.ShapeDtypeStruct((ROWS, ROWS), BF),...  72.9 us
    unnamed x1, local copies, waits for them, and re-layouts  1.57 us

profile of v2, /device:TPU:2, one launch (start us, length us, event | category | flops | bytes accessed | tf_op | source)
XLA Modules:
  0.0 74.5 jit_solution(11915462777607269887)
XLA Ops:
  0.0 72.9 %shard_map.55 = bf16[256,256]{1,0:T(8,128)(2,1)} custom-call(bf16[256,512]{1,0:T(8,128)(2,1)} %q_hbm.1, bf16[256,1024]{1,0:T(8,128)(2,1)} %k_hbm.1, bf16[256,1024]{1,0:T(8,128)(2,1)} %v_hbm.1, bf16[512,4096]{1,0:T(8,128)(2,1)} %w_hbm.1, s32[2]{0:T(128)} %order_ref.1), custom_call_target="tpu_custom_call" | custom-call | tf_op jit(solution)/shard_map/pallas_call | solution.py:381
  72.9 1.6 %copy.7 = bf16[256,256]{1,0:T(8,128)(2,1)} copy(bf16[256,256]{1,0:T(8,128)(2,1)} %shard_map.55) | data formatting | bytes 262144

commit v3 on v2

--- a/solution.py
+++ b/solution.py
@@ -33,12 +33,13 @@
 CHUNKS = [
     [("beside", 0), ("column", 1)],
     [("beside", 1)],
-    [("column", 2), ("across", 1)],
+    [("across", 0), ("column", 2)],
     [("beside", 2)],
-    [("column", 3), ("across", 2)],
+    [("across", 1), ("column", 3)],
     [("beside", 3)],
-    [("across", 3), ("column", 4), ("across", 0)],
-    [("beside", 4), ("across", 4)],
+    [("across", 2), ("column", 4)],
+    [("beside", 4), ("across", 3)],
+    [("across", 4)],
 ]
 SLOT = {(0, 0, 0): 1, (0, 0, 1): 2}
 SPANS = []
@@ -49,12 +50,15 @@
             SLOT[name] = len(SLOT) + 1
     SPANS.append((first, len(SLOT) + 1 - first))
 SLOTS = len(SLOT) + 1
+PIECES = 4
+LATE = 3
+RELAYED = (0, 1, 2, 3)
 
 
 def kernel(
     q_hbm, k_hbm, v_hbm, w_hbm, order_ref, out_ref,
     kv, vtmp, q_ref, qt, s_ref, m_ref, acc, att, wbuf,
-    keep, send1, recv1, send2, recv2, zsend, zrecv,
+    keep, send1, recv1, zsend, zrecv,
     load_sem, w_sem, send_sem, z_sem, x_sem, x2_sem, sib_sem, wx_sem, att_sem, att_sent, r_sem, r_sent, z8_sem, z8_sent,
 ):
     ctx = lax.axis_index("ctx")
@@ -83,10 +87,10 @@
     y_near = y + 1 - 2 * (y % 2)
     y_wrap = NY - 1 - y
     y_diag = (y + 2) % NY
-    y1, y2 = device(y_=y_near), device(y_=y_wrap)
+    y1, y2, y_over = device(y_=y_near), device(y_=y_wrap), device(y_=y_diag)
 
     barrier = pltpu.get_barrier_semaphore()
-    friends = [sibling, x_up, x_down, x_over, y1, y2, z_over]
+    friends = [sibling, x_up, x_down, x_over, y1, y2, y_over]
     friends += [along_z(s) for s in (1, -1, 2, -2, 3, -3, 4, -4)]
     for friend in friends:
         pl.semaphore_signal(barrier, inc=1, device_id=friend, device_id_type=MESH)
@@ -158,7 +162,8 @@
     def spread(p, j):
         send(slot(0, j, 0), slot(1, j, 0), x_sem.at[p], x_up)
         send(slot(0, j, 0), slot(2, j, 0), x_sem.at[p], x_down)
-        send(slot(0, j, 0), slot(3, j, 0), x2_sem.at[p], x_over)
+        if p not in RELAYED:
+            send(slot(0, j, 0), slot(3, j, 0), x2_sem.at[p], x_over)
 
     def share(kind, p):
         send(part(kind, p, 0), part(kind, p, 1), sib_sem.at[KINDS[kind], p], sibling)
@@ -171,6 +176,11 @@
 
     def beside_event(p):
         arrived(part("beside", p, 0), x_sem.at[p])
+        if p in RELAYED:
+            for j in GROUPS[p]:
+                keys, values = pl.ds(0, KROWS), pl.ds(KROWS, HEAD)
+                send(slot(1, j, 0).at[keys], slot(3, j, 0).at[keys], x2_sem.at[p], x_up)
+                send(slot(2, j, 0).at[values], slot(3, j, 0).at[values], x2_sem.at[p], x_down)
         share("beside", p)
 
     def across_event(p):
@@ -266,34 +276,35 @@
     own_chunk()
     column_event(1)
     beside_event(0)
-    across_event(0)
+    column_event(2)
     w_send(0)
     w_send(1)
     chunk(0)
-    column_event(2)
     beside_event(1)
+    across_event(0)
+    column_event(3)
     w_send(2)
     w_send(3)
     chunk(1)
-    column_event(3)
-    across_event(1)
+    beside_event(2)
+    column_event(4)
     w_send(4)
     w_send(5)
     chunk(2)
-    column_event(4)
-    beside_event(2)
+    across_event(1)
     w_send(6)
     w_send(7)
     chunk(3)
+    beside_event(3)
+    chunk(4)
     across_event(2)
-    chunk(4)
-    beside_event(3)
+    beside_event(4)
     chunk(5)
     across_event(3)
     chunk(6)
-    beside_event(4)
     across_event(4)
     chunk(7)
+    chunk(8)
 
     for h in range(HEADS_DEV):
         a = acc[h]
@@ -304,79 +315,56 @@
     arrived(att.at[:, 512:1024], att_sem)
 
     def product(y_, zz):
-        q = y_ * 2 + zz
-        return jnp.dot(att[...], wbuf[q], preferred_element_type=F32)
-
-    half = ROWS // 2
-    first_to = [y1, y2]
-    second_to = [y2, y1]
-
-    def first_products(n, zz):
-        d = product(y_diag, zz)
-        send1[n, 0, 1] = d[0:half].astype(BF)
-        send1[n, 1, 1] = d[half:ROWS].astype(BF)
-        a = product(y_near, zz)
-        send1[n, 0, 0] = a[0:half].astype(BF)
-        keep[n, 1, 1] = a[half:ROWS]
-        b = product(y_wrap, zz)
-        send1[n, 1, 0] = b[half:ROWS].astype(BF)
-        keep[n, 0, 1] = b[0:half]
-        c = product(y, zz)
-        keep[n, 0, 0] = c[0:half]
-        keep[n, 1, 0] = c[half:ROWS]
-
-    piece = half // 2
+        return jnp.dot(att[...], wbuf[y_ * 2 + zz], preferred_element_type=F32)
+
+    peers = [(2, y_diag, y_over), (0, y_near, y1), (1, y_wrap, y2)]
+    piece = ROWS // PIECES
 
     def rows(u):
         return pl.ds(u * piece, piece)
 
-    def first_send(n, f, u):
-        send(
-            send1.at[n, f, :, rows(u)], recv1.at[n, f, :, rows(u)], r_sem.at[0, n, f, u], first_to[f], r_sent.at[0]
-        )
-
-    def second_send(n, f, u):
-        arrived(recv1.at[n, f, :, rows(u)], r_sem.at[0, n, f, u])
-        send2[n, f, rows(u)] = (keep[n, f, 1, rows(u)] + recv1[n, f, 1, rows(u)].astype(F32)).astype(BF)
-        send(send2.at[n, f, rows(u)], recv2.at[n, f, rows(u)], r_sem.at[1, n, f, u], second_to[f], r_sent.at[1])
-
-    def column_sum(n, f, u):
-        arrived(recv2.at[n, f, rows(u)], r_sem.at[1, n, f, u])
-        return keep[n, f, 0, rows(u)] + recv1[n, f, 0, rows(u)].astype(F32) + recv2[n, f, rows(u)].astype(F32)
-
-    steps = [(f, u) for u in range(2) for f in range(2)]
-    first_products(0, zo)
-    for f, u in steps:
-        first_send(0, f, u)
-    first_products(1, zh)
-    for f, u in steps:
-        second_send(0, f, u)
-    for f, u in steps:
-        first_send(1, f, u)
-    for f, u in steps:
-        zsend[f, rows(u)] = column_sum(0, f, u).astype(BF)
-        send(zsend.at[f, rows(u)], zrecv.at[f, rows(u)], z8_sem.at[f, u], z_over, z8_sent)
-    for f, u in steps:
-        second_send(1, f, u)
-    for f, u in steps:
-        keep[1, f, 0, rows(u)] = column_sum(1, f, u)
-    for f, u in steps:
-        arrived(zrecv.at[f, rows(u)], z8_sem.at[f, u])
-        out_ref[pl.ds(f * half + u * piece, piece)] = (
-            keep[1, f, 0, rows(u)] + zrecv[f, rows(u)].astype(F32)
-        ).astype(BF)
+    def send_terms(n, u, cut):
+        part_rows = pl.ds(u * (ROWS // cut), ROWS // cut)
+        for i, _, target in peers:
+            send(send1.at[n, i, part_rows], recv1.at[n, i, part_rows], r_sem.at[n, u], target, r_sent)
+
+    for i, y_, _ in peers:
+        send1[0, i] = product(y_, zo).astype(BF)
+    for u in range(PIECES):
+        send_terms(0, u, PIECES)
+    keep[0] = product(y, zo)
+    for i, y_, _ in peers:
+        send1[1, i] = product(y_, zh).astype(BF)
+    keep[1] = product(y, zh)
+
+    for u in range(PIECES):
+        arrived(recv1.at[0, :, rows(u)], r_sem.at[0, u])
+        total = keep[0, rows(u)]
+        for i in range(3):
+            total = total + recv1[0, i, rows(u)].astype(F32)
+        zsend[rows(u)] = total.astype(BF)
+        send(zsend.at[rows(u)], zrecv.at[rows(u)], z8_sem.at[u], z_over, z8_sent)
+        if u == LATE:
+            send_terms(1, 0, 1)
+    arrived(recv1.at[1], r_sem.at[1, 0])
+    for u in range(PIECES):
+        total = keep[1, rows(u)]
+        for i in range(3):
+            total = total + recv1[1, i, rows(u)].astype(F32)
+        keep[1, rows(u)] = total
+    for u in range(PIECES):
+        arrived(zrecv.at[rows(u)], z8_sem.at[u])
+        out_ref[rows(u)] = (keep[1, rows(u)] + zrecv[rows(u)].astype(F32)).astype(BF)
 
     landed(kv.at[pl.ds(0, 62)], send_sem).wait_send()
     landed(wbuf.at[:, 512:1024], wx_sem.at[1]).wait_send()
     landed(att.at[:, 0:512], att_sent).wait_send()
-    landed(send1, r_sent.at[0]).wait_send()
-    landed(send2, r_sent.at[1]).wait_send()
+    landed(send1, r_sent).wait_send()
     landed(zsend, z8_sent).wait_send()
 
 
 def shards(queries, keys, values, out_weight, block_order):
     any_spec = pl.BlockSpec(memory_space=pl.ANY)
-    half = ROWS // 2
     dma = pltpu.SemaphoreType.DMA
     return pl.pallas_call(
         kernel,
@@ -393,13 +381,11 @@
             pltpu.VMEM((HEADS_DEV, HEAD + 16, ROWS), F32),
             pltpu.VMEM((ROWS, 1024), BF),
             pltpu.VMEM((8, 1024, ROWS), BF),
-            pltpu.VMEM((2, 2, 2, half, ROWS), F32),
-            pltpu.VMEM((2, 2, 2, half, ROWS), BF),
-            pltpu.VMEM((2, 2, 2, half, ROWS), BF),
-            pltpu.VMEM((2, 2, half, ROWS), BF),
-            pltpu.VMEM((2, 2, half, ROWS), BF),
-            pltpu.VMEM((2, half, ROWS), BF),
-            pltpu.VMEM((2, half, ROWS), BF),
+            pltpu.VMEM((2, ROWS, ROWS), F32),
+            pltpu.VMEM((2, 3, ROWS, ROWS), BF),
+            pltpu.VMEM((2, 3, ROWS, ROWS), BF),
+            pltpu.VMEM((ROWS, ROWS), BF),
+            pltpu.VMEM((ROWS, ROWS), BF),
             dma((7,)),
             dma,
             dma,
@@ -410,9 +396,9 @@
             dma((2,)),
             dma,
             dma,
-            dma((2, 2, 2, 2)),
-            dma((2,)),
-            dma((2, 2)),
+            dma((2, PIECES)),
+            dma,
+            dma((PIECES,)),
             dma,
         ],
         compiler_params=pltpu.CompilerParams(

time: 74.6 us -> 70.6 us (0.946)
  the two profiles are of different devices: /device:TPU:2 before, /device:TPU:1 now
where the time goes in v3:
time: 70.6 us; the launch traced here: 70.4 us
  Pallas kernels  68.8 us (97%)
  local copies, waits for them, and re-layouts  1.57 us (2%)
    pallas_call x1, Pallas kernels, shards(): pl.pallas_call(kernel, out_shape=jax.ShapeDtypeStruct((ROWS, ROWS), BF),...  68.8 us
    unnamed x1, local copies, waits for them, and re-layouts  1.57 us

profile of v3, /device:TPU:1, one launch (start us, length us, event | category | flops | bytes accessed | tf_op | source)
XLA Modules:
  0.0 70.4 jit_solution(16642999239567382421)
XLA Ops:
  0.0 68.8 %shard_map.55 = bf16[256,256]{1,0:T(8,128)(2,1)} custom-call(bf16[256,512]{1,0:T(8,128)(2,1)} %q_hbm.1, bf16[256,1024]{1,0:T(8,128)(2,1)} %k_hbm.1, bf16[256,1024]{1,0:T(8,128)(2,1)} %v_hbm.1, bf16[512,4096]{1,0:T(8,128)(2,1)} %w_hbm.1, s32[2]{0:T(128)} %order_ref.1), custom_call_target="tpu_custom_call" | custom-call | tf_op jit(solution)/shard_map/pallas_call | solution.py:369
  68.9 1.6 %copy.7 = bf16[256,256]{1,0:T(8,128)(2,1)} copy(bf16[256,256]{1,0:T(8,128)(2,1)} %shard_map.55) | data formatting | bytes 262144

commit v4 on v3

--- a/solution.py
+++ b/solution.py
@@ -91,7 +91,7 @@
 
     barrier = pltpu.get_barrier_semaphore()
     friends = [sibling, x_up, x_down, x_over, y1, y2, y_over]
-    friends += [along_z(s) for s in (1, -1, 2, -2, 3, -3, 4, -4)]
+    friends += [along_z(s) for s in (1, -1, 2, -2)]
     for friend in friends:
         pl.semaphore_signal(barrier, inc=1, device_id=friend, device_id_type=MESH)
 
@@ -267,16 +267,19 @@
     spread(0, 0)
     right(2)
     left(2)
-    right(3)
-    left(3)
-    send(for_step(4).at[0:KROWS], slot(0, 7, 0).at[0:KROWS], z_sem.at[7], along_z(4))
-    send(for_step(-4).at[KROWS:SLOT_ROWS], slot(0, 7, 0).at[KROWS:SLOT_ROWS], z_sem.at[7], along_z(-4))
+
+    def farthest():
+        send(for_step(4).at[0:KROWS], slot(0, 7, 0).at[0:KROWS], z_sem.at[7], along_z(4))
+        send(for_step(-4).at[KROWS:SLOT_ROWS], slot(0, 7, 0).at[KROWS:SLOT_ROWS], z_sem.at[7], along_z(-4))
 
     prepare_queries()
     own_chunk()
     column_event(1)
+    right(3)
+    left(3)
     beside_event(0)
     column_event(2)
+    farthest()
     w_send(0)
     w_send(1)
     chunk(0)
@@ -368,7 +371,7 @@
     dma = pltpu.SemaphoreType.DMA
     return pl.pallas_call(
         kernel,
-        out_shape=jax.ShapeDtypeStruct((ROWS, ROWS), BF),
+        out_shape=pltpu.VMEM((ROWS, ROWS), BF),
         in_specs=[any_spec] * 4 + [pl.BlockSpec(memory_space=pltpu.SMEM)],
         out_specs=pl.BlockSpec(memory_space=pltpu.VMEM),
         scratch_shapes=[

time: 70.6 us -> 65.1 us (0.922); the launches traced: 70.4 us -> 64 us
  Pallas kernels: 68.8 us -> 63.4 us
  local copies, waits for them, and re-layouts: 1.57 us -> 0.66 us
    pallas_call x1, Pallas kernels: 68.8 us -> 63.4 us  [shards(): pl.pallas_call(kernel, out_shape=pltpu.VMEM((ROWS, ROWS), BF), in_specs=[...]
    unnamed x1, local copies, waits for them, and re-layouts: 1.57 us -> 0.66 us
where the time goes in v4:
time: 65.1 us; the launch traced here: 64 us
  Pallas kernels  63.4 us (97%)
  local copies, waits for them, and re-layouts  0.66 us (1%)
    pallas_call x1, Pallas kernels, shards(): pl.pallas_call(kernel, out_shape=pltpu.VMEM((ROWS, ROWS), BF), in_specs=[...  63.4 us

profile of v4, /device:TPU:1, one launch (start us, length us, event | category | flops | bytes accessed | tf_op | source)
XLA Modules:
  0.0 64.0 jit_solution(14750621050949352394)
XLA Ops:
  0.0 63.4 %shard_map.55 = bf16[256,256]{1,0:T(8,128)(2,1)S(1)} custom-call(bf16[256,512]{1,0:T(8,128)(2,1)} %q_hbm.1, bf16[256,1024]{1,0:T(8,128)(2,1)} %k_hbm.1, bf16[256,1024]{1,0:T(8,128)(2,1)} %v_hbm.1, bf16[512,4096]{1,0:T(8,128)(2,1)} %w_hbm.1, s32[2]{0:T(128)} %order_ref.1), custom_call_target="tpu_custom_call" | custom-call | tf_op jit(solution)/shard_map/pallas_call | solution.py:372
  63.4 0.7 %copy.7 = bf16[256,256]{1,0:T(8,128)(2,1)} copy(bf16[256,256]{1,0:T(8,128)(2,1)S(1)} %shard_map.55) | data formatting | bytes 262144

commit v5 on v4

--- a/solution.py
+++ b/solution.py
@@ -50,7 +50,7 @@
             SLOT[name] = len(SLOT) + 1
     SPANS.append((first, len(SLOT) + 1 - first))
 SLOTS = len(SLOT) + 1
-PIECES = 4
+PIECES = 8
 LATE = 3
 RELAYED = (0, 1, 2, 3)
 
@@ -273,11 +273,11 @@
         send(for_step(-4).at[KROWS:SLOT_ROWS], slot(0, 7, 0).at[KROWS:SLOT_ROWS], z_sem.at[7], along_z(-4))
 
     prepare_queries()
-    own_chunk()
     column_event(1)
     right(3)
     left(3)
     beside_event(0)
+    own_chunk()
     column_event(2)
     farthest()
     w_send(0)

time: 65.1 us -> 64 us (0.983); the launches traced: 64 us -> 63.8 us
  no operation moved by 1% of the time
where the time goes in v5:
time: 64 us; the launch traced here: 63.8 us
  Pallas kernels  63.2 us (99%)
  local copies, waits for them, and re-layouts  0.66 us (1%)
    pallas_call x1, Pallas kernels, shards(): pl.pallas_call(kernel, out_shape=pltpu.VMEM((ROWS, ROWS), BF), in_specs=[...  63.2 us

profile of v5, /device:TPU:1, one launch (start us, length us, event | category | flops | bytes accessed | tf_op | source)
XLA Modules:
  0.0 63.8 jit_solution(16168855543671063111)
XLA Ops:
  0.0 63.2 %shard_map.55 = bf16[256,256]{1,0:T(8,128)(2,1)S(1)} custom-call(bf16[256,512]{1,0:T(8,128)(2,1)} %q_hbm.1, bf16[256,1024]{1,0:T(8,128)(2,1)} %k_hbm.1, bf16[256,1024]{1,0:T(8,128)(2,1)} %v_hbm.1, bf16[512,4096]{1,0:T(8,128)(2,1)} %w_hbm.1, s32[2]{0:T(128)} %order_ref.1), custom_call_target="tpu_custom_call" | custom-call | tf_op jit(solution)/shard_map/pallas_call | solution.py:372
  63.2 0.7 %copy.7 = bf16[256,256]{1,0:T(8,128)(2,1)} copy(bf16[256,256]{1,0:T(8,128)(2,1)S(1)} %shard_map.55) | data formatting | bytes 262144
